TPU v7x, 32 devices: a 4x4x1 block of a 4x4x8 slice. The times are simulated.
32 devices in a mesh: dp: 1 (over z), ei: 4 (over y), eo: 8 (over x, core).
Axes of the slice: x: 4, y: 4, z: 1, core: 2. Of those that a mesh axis runs over, the one named last changes fastest.
The devices are a block of a 4x4x8 slice.
Arguments:
- tokens: bfloat16 [6144, 2048], P(('dp', 'ei', 'eo'))
- expert_idx: int32 [6144, 8], P(('dp', 'ei', 'eo'))
- gates: float32 [6144, 8], P(('dp', 'ei', 'eo'))
- w_gate: bfloat16 [32, 2048, 1024], P(('ei', 'eo'))
- w_up: bfloat16 [32, 2048, 1024], P(('ei', 'eo'))
- w_down: bfloat16 [32, 1024, 2048], P(('ei', 'eo'))
- grad_out: bfloat16 [6144, 2048], P(('dp', 'ei', 'eo'))
Outputs:
- output 1: bfloat16 [6144, 2048], P(('dp', 'ei', 'eo'))
- output 2: bfloat16 [6144, 2048], P(('dp', 'ei', 'eo'))
- output 3: float32 [6144, 8], P(('dp', 'ei', 'eo'))
- output 4: bfloat16 [32, 2048, 1024], P(('dp', 'ei', 'eo'))
- output 5: bfloat16 [32, 2048, 1024], P(('dp', 'ei', 'eo'))
- output 6: bfloat16 [32, 1024, 2048], P(('dp', 'ei', 'eo'))
All inputs are finite; a program needn't handle non-finite values.
Results may differ from a plain program's by a relative error of at most 0.00784686.
Values are sent between devices in bfloat16 or wider.
A program may use at most 768 MiB of HBM per device.

v0:
```python
import jax
import jax.numpy as jnp
from jax import lax
from jax.sharding import PartitionSpec as P


def slot_tables(flat_ids, num_experts, capacity):
    n_assign = flat_ids.shape[0]
    sort_order = jnp.argsort(flat_ids, stable=True).astype(jnp.int32)
    sorted_ids = flat_ids[sort_order]
    counts = jnp.zeros((num_experts,), jnp.int32).at[flat_ids].add(1)
    starts = jnp.cumsum(counts) - counts
    slot_sorted = sorted_ids * capacity + jnp.arange(n_assign, dtype=jnp.int32) - starts[sorted_ids]
    slot_of = jnp.zeros((n_assign,), jnp.int32).at[sort_order].set(slot_sorted)
    filler = jnp.full((num_experts * capacity,), n_assign, jnp.int32).at[slot_sorted].set(sort_order)
    return slot_of, filler


def exchange(buffer, ei_size, eo_size):
    row_shape = buffer.shape[1:]
    peer_grid = buffer.reshape((ei_size, eo_size) + row_shape)
    peer_grid = lax.all_to_all(peer_grid, 'eo', 1, 1, tiled=True)
    peer_grid = lax.all_to_all(peer_grid, 'ei', 0, 0, tiled=True)
    return peer_grid.reshape(buffer.shape)


def solution(mesh):
    ei_size = mesh.shape['ei']
    eo_size = mesh.shape['eo']
    group_size = ei_size * eo_size
    tok_spec = P(('dp', 'ei', 'eo'))
    exp_spec = P(('ei', 'eo'))

    def device_step(tok_loc, idx_loc, gate_loc, w_gate, w_up, w_down, dy_loc):
        tok_dev, top_k = idx_loc.shape
        exp_dev, d_model, d_ff = w_gate.shape
        num_experts = exp_dev * group_size
        capacity = min(tok_dev, tok_dev * top_k // (4 * exp_dev))
        send_rows = exp_dev * capacity
        slot_of, filler = slot_tables(idx_loc.reshape(-1), num_experts, capacity)
        tok_ids = filler // top_k
        zero_row = jnp.zeros((1, d_model), jnp.bfloat16)
        send_x = jnp.concatenate([tok_loc, zero_row])[tok_ids].reshape(group_size, send_rows, d_model)
        x_recv = exchange(send_x, ei_size, eo_size).reshape(group_size, exp_dev, capacity, d_model)
        h_gate = jnp.einsum('secd,edf->secf', x_recv, w_gate, preferred_element_type=jnp.float32)
        h_up = jnp.einsum('secd,edf->secf', x_recv, w_up, preferred_element_type=jnp.float32)
        sig_gate = jax.nn.sigmoid(h_gate)
        hidden = (h_gate * sig_gate * h_up).astype(jnp.bfloat16)
        y_expert = jnp.einsum('secf,efd->secd', hidden, w_down, preferred_element_type=jnp.float32).astype(jnp.bfloat16)
        y_back = exchange(y_expert.reshape(group_size, send_rows, d_model), ei_size, eo_size)
        y_rows = y_back.reshape(num_experts * capacity, d_model)[slot_of].reshape(tok_dev, top_k, d_model)
        layer_out = jnp.sum(gate_loc[:, :, None] * y_rows, axis=1).astype(jnp.bfloat16)
        grad_gates = jnp.einsum('tkd,td->tk', y_rows, dy_loc, preferred_element_type=jnp.float32)
        gate_slot = jnp.concatenate([gate_loc.reshape(-1), jnp.zeros((1,), jnp.float32)])[filler]
        dy_slot = jnp.concatenate([dy_loc, zero_row])[tok_ids]
        send_dy = (gate_slot[:, None] * dy_slot).astype(jnp.bfloat16).reshape(group_size, send_rows, d_model)
        dy_recv = exchange(send_dy, ei_size, eo_size).reshape(group_size, exp_dev, capacity, d_model)
        d_hidden = jnp.einsum('secd,efd->secf', dy_recv, w_down, preferred_element_type=jnp.float32)
        d_up = (d_hidden * h_gate * sig_gate).astype(jnp.bfloat16)
        d_gate = (d_hidden * h_up * sig_gate * (1.0 + h_gate * (1.0 - sig_gate))).astype(jnp.bfloat16)
        dx_expert = (jnp.einsum('secf,edf->secd', d_gate, w_gate, preferred_element_type=jnp.float32) + jnp.einsum('secf,edf->secd', d_up, w_up, preferred_element_type=jnp.float32)).astype(jnp.bfloat16)
        grad_w_gate = jnp.einsum('secd,secf->edf', x_recv, d_gate, preferred_element_type=jnp.float32).astype(jnp.bfloat16)
        grad_w_up = jnp.einsum('secd,secf->edf', x_recv, d_up, preferred_element_type=jnp.float32).astype(jnp.bfloat16)
        grad_w_down = jnp.einsum('secf,secd->efd', hidden, dy_recv, preferred_element_type=jnp.float32).astype(jnp.bfloat16)
        dx_back = exchange(dx_expert.reshape(group_size, send_rows, d_model), ei_size, eo_size)
        dx_rows = dx_back.reshape(num_experts * capacity, d_model)[slot_of].reshape(tok_dev, top_k, d_model)
        grad_tokens = jnp.sum(dx_rows.astype(jnp.float32), axis=1).astype(jnp.bfloat16)
        return layer_out, grad_tokens, grad_gates, grad_w_gate, grad_w_up, grad_w_down

    return jax.shard_map(device_step, mesh=mesh, in_specs=(tok_spec, tok_spec, tok_spec, exp_spec, exp_spec, exp_spec, tok_spec), out_specs=(tok_spec, tok_spec, tok_spec, tok_spec, tok_spec, tok_spec), check_vma=False)
```

profile of v0, /device:TPU:97, one launch (start us, length us, event | category | flops | bytes accessed | tf_op | source)
XLA Modules:
  0.0 2493.8 jit_solution(7188895628061183282)
XLA Ops:
  57.2 30.9 %gather_fusion.1 = bf16[6144,2048]{1,0:T(8,128)(2,1)} fusion(bf16[193,2048]{1,0:T(8,128)(2,1)S(1)} %concatenate.9, s32[6144]{0:T(1024)S(1)} %get-tuple-element.41), kind=kCustom, calls=%fused_computation.1 | custom fusion | bytes 50356224 | tf_op jit(solution)/shard_map/gather | solution.py:43
  118.5 34.3 %gather_fusion.3 = f32[6144]{0:T(1024)S(1)} fusion(f32[1537]{0:T(1024)S(1)} %pad_maximum_fusion, s32[6144]{0:T(1024)S(1)} %get-tuple-element.40), kind=kCustom, calls=%fused_computation.3 | custom fusion | bytes 73728 | tf_op jit(solution)/shard_map/gather | solution.py:54
  153.0 31.0 %gather_fusion.4 = bf16[6144,2048]{1,0:T(8,128)(2,1)} fusion(bf16[193,2048]{1,0:T(8,128)(2,1)S(1)} %concatenate.11, s32[6144]{0:T(1024)S(1)} %get-tuple-element.41), kind=kCustom, calls=%fused_computation.4 | custom fusion | bytes 50356224 | tf_op jit(solution)/shard_map/gather | solution.py:55
  184.0 21.9 fusion
  205.8 185.2 %all-to-all-done = bf16[4,8,192,2048]{3,2,0,1:T(8,128)(2,1)} async-done(((bf16[4,8,192,2048]{3,2,0,1:T(8,128)(2,1)}), bf16[4,8,192,2048]{3,2,0,1:T(8,128)(2,1)}, u32[]{:S(2)}, u32[]{:S(2)}) %all-to-all-start) | async-done | bytes 25165856 | tf_op jit(solution)/shard_map/all_to_all | solution.py:22
  419.6 252.3 %all-to-all-done.4 = bf16[4,8,192,2048]{3,2,0,1:T(8,128)(2,1)} async-done(((bf16[4,8,192,2048]{3,2,0,1:T(8,128)(2,1)}), bf16[4,8,192,2048]{3,2,0,1:T(8,128)(2,1)}, u32[]{:S(2)}, u32[]{:S(2)}) %all-to-all-start.4) | async-done | bytes 25165856 | tf_op jit(solution)/shard_map/all_to_all | solution.py:22
  701.4 252.3 %all-to-all-done.1 = bf16[4,8,192,2048]{3,2,1,0:T(8,128)(2,1)} async-done(((bf16[4,8,192,2048]{3,2,1,0:T(8,128)(2,1)}), bf16[4,8,192,2048]{3,2,1,0:T(8,128)(2,1)}, u32[]{:S(2)}, u32[]{:S(2)}) %all-to-all-start.1) | async-done | bytes 25165856 | tf_op jit(solution)/shard_map/all_to_all | solution.py:23
  962.8 32.7 %fusion.33 = f32[32,192,1024]{2,1,0:T(8,128)} fusion(bf16[32,192,2048]{2,1,0:T(8,128)(2,1)} %bitcast.34, bf16[1,2048,1024]{2,1,0:T(8,128)(2,1)} %param.11), kind=kOutput, calls=%fused_computation.50 | convolution fusion | flops 25769803776 | bytes 54525952 | tf_op jit(solution)/shard_map/secd,edf->secf/dot_general | solution.py:46
  995.4 31.3 %fusion.36 = f32[32,192,1024]{2,1,0:T(8,128)} fusion(bf16[32,192,2048]{2,1,0:T(8,128)(2,1)} %bitcast.34, bf16[1,2048,1024]{2,1,0:T(8,128)(2,1)S(1)} %copy-done.6), kind=kOutput, calls=%fused_computation.53 | convolution fusion | flops 25769803776 | bytes 54525952 | tf_op jit(solution)/shard_map/secd,edf->secf/dot_general | solution.py:45
  1026.8 207.6 %all-to-all-done.5 = bf16[4,8,192,2048]{3,2,1,0:T(8,128)(2,1)} async-done(((bf16[4,8,192,2048]{3,2,1,0:T(8,128)(2,1)}), bf16[4,8,192,2048]{3,2,1,0:T(8,128)(2,1)}, u32[]{:S(2)}, u32[]{:S(2)}) %all-to-all-start.5) | async-done | bytes 25165856 | tf_op jit(solution)/shard_map/all_to_all | solution.py:23
  1234.4 46.7 %fusion.5 = (bf16[32,1,192,1024]{3,2,0,1:T(8,128)(2,1)}, bf16[32,1,192,1024]{3,2,0,1:T(8,128)(2,1)}, bf16[32,1,192,1024]{3,2,0,1:T(8,128)(2,1)}) fusion(f32[32,192,1024]{2,1,0:T(8,128)} %fusion.36, f32[32,192,1024]{2,1,0:T(8,128)} %fusion.33, bf16[32,192,2048]{2,1,0:T(8,128)(2,1)} %bitcast.57, bf16[1,1024,2048]{2,1,0:T(8,128)(2,1)} %param.12), kind=kOutput, calls=%fused_computation.18 | convolution fusion | flops 25870467072 | bytes 117440512 | tf_op jit(solution)/shard_map/secd,efd->secf/dot_general | solution.py:58
  1281.1 33.6 %convolution_convert_fusion = bf16[32,192,2048]{2,1,0:T(8,128)(2,1)} fusion(bf16[32,1,192,1024]{3,2,0,1:T(8,128)(2,1)} %get-tuple-element.39, bf16[1,1024,2048]{2,1,0:T(8,128)(2,1)} %param.12), kind=kOutput, calls=%fused_computation.28 | convolution fusion | flops 25782386688 | bytes 41943040 | tf_op jit(solution)/shard_map/secf,efd->secd/dot_general | solution.py:49
  1314.7 21.1 copy.53
  1345.2 34.9 %fusion.16 = f32[32,192,2048]{2,1,0:T(8,128)} fusion(bf16[32,1,192,1024]{3,2,0,1:T(8,128)(2,1)} %get-tuple-element.38, bf16[1,2048,1024]{2,1,0:T(8,128)(2,1)} %param.10), kind=kOutput, calls=%fused_computation.34 | convolution fusion | flops 25769803776 | bytes 67108864 | tf_op jit(solution)/shard_map/secf,edf->secd/dot_general | solution.py:61
  1380.1 37.7 %add_convert_fusion = bf16[32,192,2048]{2,1,0:T(8,128)(2,1)} fusion(f32[32,192,2048]{2,1,0:T(8,128)} %fusion.16, bf16[32,1,192,1024]{3,2,0,1:T(8,128)(2,1)} %get-tuple-element.37, bf16[1,2048,1024]{2,1,0:T(8,128)(2,1)S(1)} %copy-done.7), kind=kOutput, calls=%fused_computation.11 | convolution fusion | flops 25794969600 | bytes 92274688 | tf_op jit(solution)/shard_map/secf,edf->secd/dot_general | solution.py:61
  1438.8 179.6 %all-to-all-done.2 = bf16[4,8,192,2048]{3,2,0,1:T(8,128)(2,1)} async-done(((bf16[4,8,192,2048]{3,2,0,1:T(8,128)(2,1)}), bf16[4,8,192,2048]{3,2,0,1:T(8,128)(2,1)}, u32[]{:S(2)}, u32[]{:S(2)}) %all-to-all-start.2) | async-done | bytes 25165856 | tf_op jit(solution)/shard_map/all_to_all | solution.py:22
  1646.8 252.4 %all-to-all-done.6 = bf16[4,8,192,2048]{3,2,0,1:T(8,128)(2,1)} async-done(((bf16[4,8,192,2048]{3,2,0,1:T(8,128)(2,1)}), bf16[4,8,192,2048]{3,2,0,1:T(8,128)(2,1)}, u32[]{:S(2)}, u32[]{:S(2)}) %all-to-all-start.6) | async-done | bytes 25165856 | tf_op jit(solution)/shard_map/all_to_all | solution.py:22
  1928.8 251.3 %all-to-all-done.3 = bf16[4,8,192,2048]{3,2,1,0:T(8,128)(2,1)} async-done(((bf16[4,8,192,2048]{3,2,1,0:T(8,128)(2,1)}), bf16[4,8,192,2048]{3,2,1,0:T(8,128)(2,1)}, u32[]{:S(2)}, u32[]{:S(2)}) %all-to-all-start.3) | async-done | bytes 25165856 | tf_op jit(solution)/shard_map/all_to_all | solution.py:23
  2195.3 34.3 %fusion.44 = bf16[1,1024,2048]{2,1,0:T(8,128)(2,1)} fusion(bf16[32,192,2048]{2,1,0:T(8,128)(2,1)} %bitcast.57, bf16[32,1,192,1024]{3,2,0,1:T(8,128)(2,1)} %get-tuple-element.39), kind=kOutput, calls=%fused_computation.57 | convolution fusion | flops 25771900928 | bytes 41943040 | tf_op jit(solution)/shard_map/secf,secd->efd/dot_general | solution.py:64
  2229.6 34.2 %fusion.41 = bf16[1,2048,1024]{2,1,0:T(8,128)(2,1)} fusion(bf16[32,192,2048]{2,1,0:T(8,128)(2,1)} %bitcast.34, bf16[32,1,192,1024]{3,2,0,1:T(8,128)(2,1)} %get-tuple-element.37), kind=kOutput, calls=%fused_computation.56 | convolution fusion | flops 25771900928 | bytes 41943040 | tf_op jit(solution)/shard_map/secd,secf->edf/dot_general | solution.py:63
  2263.8 30.9 %fusion.38 = bf16[1,2048,1024]{2,1,0:T(8,128)(2,1)} fusion(bf16[32,192,2048]{2,1,0:T(8,128)(2,1)} %bitcast.34, bf16[32,1,192,1024]{3,2,0,1:T(8,128)(2,1)S(1)} %bitcast.196), kind=kOutput, calls=%fused_computation.55 | convolution fusion | flops 25771900928 | bytes 41943040 | tf_op jit(solution)/shard_map/secd,secf->edf/dot_general | solution.py:62
  2294.8 24.3 gather_fusion.2
  2336.7 123.6 %all-to-all-done.7 = bf16[4,8,192,2048]{3,2,1,0:T(8,128)(2,1)} async-done(((bf16[4,8,192,2048]{3,2,1,0:T(8,128)(2,1)}), bf16[4,8,192,2048]{3,2,1,0:T(8,128)(2,1)}, u32[]{:S(2)}, u32[]{:S(2)}) %all-to-all-start.7) | async-done | bytes 25165856 | tf_op jit(solution)/shard_map/all_to_all | solution.py:23
  2460.3 24.4 gather_fusion.5
  (74 shorter events, 283.9 us)
Async XLA Ops:
  19.6 0.6 copy-start.4
  109.2 8.5 copy-start.5
  109.2 281.9 %all-to-all-start = ((bf16[4,8,192,2048]{3,2,0,1:T(8,128)(2,1)}), bf16[4,8,192,2048]{3,2,0,1:T(8,128)(2,1)}, u32[]{:S(2)}, u32[]{:S(2)}) async-start(bf16[4,8,192,2048]{3,2,0,1:T(8,128)(2,1)} %copy.51), calls=%async_computation | async-start | bytes 50331648 | tf_op jit(solution)/shard_map/all_to_all | solution.py:22
  117.7 35.3 %copy-start.2 = (bf16[192,2048]{1,0:T(8,128)(2,1)S(1)}, bf16[192,2048]{1,0:T(8,128)(2,1)}, u32[]{:S(2)}) copy-start(bf16[192,2048]{1,0:T(8,128)(2,1)} %param.13) | copy-start | bytes 2359300
  117.8 0.6 copy-start
  391.0 280.9 %all-to-all-start.4 = ((bf16[4,8,192,2048]{3,2,0,1:T(8,128)(2,1)}), bf16[4,8,192,2048]{3,2,0,1:T(8,128)(2,1)}, u32[]{:S(2)}, u32[]{:S(2)}) async-start(bf16[4,8,192,2048]{3,2,0,1:T(8,128)(2,1)} %fusion), calls=%async_computation.4 | async-start | bytes 50331648 | tf_op jit(solution)/shard_map/all_to_all | solution.py:22
  671.9 281.8 %all-to-all-start.1 = ((bf16[4,8,192,2048]{3,2,1,0:T(8,128)(2,1)}), bf16[4,8,192,2048]{3,2,1,0:T(8,128)(2,1)}, u32[]{:S(2)}, u32[]{:S(2)}) async-start(bf16[4,8,192,2048]{3,2,1,0:T(8,128)(2,1)} %copy.52), calls=%async_computation.1 | async-start | bytes 50331648 | tf_op jit(solution)/shard_map/all_to_all | solution.py:23
  953.7 280.7 %all-to-all-start.5 = ((bf16[4,8,192,2048]{3,2,1,0:T(8,128)(2,1)}), bf16[4,8,192,2048]{3,2,1,0:T(8,128)(2,1)}, u32[]{:S(2)}, u32[]{:S(2)}) async-start(bf16[4,8,192,2048]{3,2,1,0:T(8,128)(2,1)} %copy.58), calls=%async_computation.5 | async-start | bytes 50331648 | tf_op jit(solution)/shard_map/all_to_all | solution.py:23
  962.8 32.7 %copy-start.6 = (bf16[1,2048,1024]{2,1,0:T(8,128)(2,1)S(1)}, bf16[1,2048,1024]{2,1,0:T(8,128)(2,1)}, u32[]{:S(2)}) copy-start(bf16[1,2048,1024]{2,1,0:T(8,128)(2,1)} %param.10) | copy-start | bytes 12582916
  1335.8 282.6 %all-to-all-start.2 = ((bf16[4,8,192,2048]{3,2,0,1:T(8,128)(2,1)}), bf16[4,8,192,2048]{3,2,0,1:T(8,128)(2,1)}, u32[]{:S(2)}, u32[]{:S(2)}) async-start(bf16[4,8,192,2048]{3,2,0,1:T(8,128)(2,1)} %copy.53), calls=%async_computation.2 | async-start | bytes 50331648 | tf_op jit(solution)/shard_map/all_to_all | solution.py:22
  1345.2 34.9 %copy-start.7 = (bf16[1,2048,1024]{2,1,0:T(8,128)(2,1)S(1)}, bf16[1,2048,1024]{2,1,0:T(8,128)(2,1)}, u32[]{:S(2)}) copy-start(bf16[1,2048,1024]{2,1,0:T(8,128)(2,1)} %param.11) | copy-start | bytes 12582916
  1618.4 280.7 %all-to-all-start.6 = ((bf16[4,8,192,2048]{3,2,0,1:T(8,128)(2,1)}), bf16[4,8,192,2048]{3,2,0,1:T(8,128)(2,1)}, u32[]{:S(2)}, u32[]{:S(2)}) async-start(bf16[4,8,192,2048]{3,2,0,1:T(8,128)(2,1)} %copy.59), calls=%async_computation.6 | async-start | bytes 50331648 | tf_op jit(solution)/shard_map/all_to_all | solution.py:22
  1899.2 280.9 %all-to-all-start.3 = ((bf16[4,8,192,2048]{3,2,1,0:T(8,128)(2,1)}), bf16[4,8,192,2048]{3,2,1,0:T(8,128)(2,1)}, u32[]{:S(2)}, u32[]{:S(2)}) async-start(bf16[4,8,192,2048]{3,2,1,0:T(8,128)(2,1)} %copy.54), calls=%async_computation.3 | async-start | bytes 50331648 | tf_op jit(solution)/shard_map/all_to_all | solution.py:23
  2180.1 280.2 %all-to-all-start.7 = ((bf16[4,8,192,2048]{3,2,1,0:T(8,128)(2,1)}), bf16[4,8,192,2048]{3,2,1,0:T(8,128)(2,1)}, u32[]{:S(2)}, u32[]{:S(2)}) async-start(bf16[4,8,192,2048]{3,2,1,0:T(8,128)(2,1)} %copy.60), calls=%async_computation.7 | async-start | bytes 50331648 | tf_op jit(solution)/shard_map/all_to_all | solution.py:23
  2195.3 68.5 %slice-start = ((s8[12582912]{0:T(1024)(128)(4,1)}), s8[4194304]{0:T(1024)(128)(4,1)S(1)}, s32[]{:S(2)}) async-start(s8[12582912]{0:T(1024)(128)(4,1)} %bitcast.195), calls=%async_computation.8 | async-start | bytes 8388608
  2195.3 68.5 %slice-start.1 = ((s8[12582912]{0:T(1024)(128)(4,1)}), s8[4194304]{0:T(1024)(128)(4,1)S(1)}, s32[]{:S(2)}) async-start(s8[12582912]{0:T(1024)(128)(4,1)} %bitcast.195), calls=%async_computation.9 | async-start | bytes 8388608
  2229.6 34.2 %slice-start.2 = ((s8[12582912]{0:T(1024)(128)(4,1)}), s8[4194304]{0:T(1024)(128)(4,1)S(1)}, s32[]{:S(2)}) async-start(s8[12582912]{0:T(1024)(128)(4,1)} %bitcast.195), calls=%async_computation.10 | async-start | bytes 8388608
  2294.7 24.3 copy-start.3
  2294.7 31.8 %copy-start.1 = (f32[192,8]{1,0:T(8,128)S(1)}, f32[192,8]{1,0:T(8,128)}, u32[]{:S(2)}) copy-start(f32[192,8]{1,0:T(8,128)} %copy-done) | copy-start | bytes 18436
where the time goes:
time: 2500 us; the launch traced here: 2490 us
  waiting for transfers between devices  1700 us (68%)
  matrix products  323 us (13%)
  local copies, waits for them, and re-layouts  319 us (13%)
  other arithmetic  78.3 us (3%)
  starting transfers between devices  67.6 us (3%)
    all_to_all x4, waiting for transfers between devices, exchange(): peer_grid = lax.all_to_all(peer_grid, 'eo', 1, 1, tiled=True)  870 us
    all_to_all x4, waiting for transfers between devices, exchange(): peer_grid = lax.all_to_all(peer_grid, 'ei', 0, 0, tiled=True)  835 us
    all_to_all x4, local copies, waits for them, and re-layouts, exchange(): peer_grid = lax.all_to_all(peer_grid, 'eo', 1, 1, tiled=True)  84.1 us
    another operation x3, local copies, waits for them, and re-layouts, exchange(): peer_grid = buffer.reshape((ei_size, eo_size) + row_shape)  63.1 us
  transfers between devices with their start and end apart: 8, of which 8 were waited for; matrix products, arithmetic and copies ran while one was open for 19% of the time, Pallas kernels for 0%

commit v1 on v0

v1 whole, which is shorter than its diff:
```python
import jax
import jax.numpy as jnp
from jax import lax
from jax.sharding import PartitionSpec as P

GROUP = ('ei', 'eo')


def solution(mesh):
    eo_size = mesh.shape['eo']
    tok_spec = P(('dp', 'ei', 'eo'))
    exp_spec = P(('ei', 'eo'))
    f32, bf16 = jnp.float32, jnp.bfloat16

    def dot(x, y, dims):
        return lax.dot_general(x, y, (dims, ((), ())), preferred_element_type=f32)

    def device_step(tok_loc, idx_loc, gate_loc, w_gate, w_up, w_down, dy_loc):
        tok_dev = tok_loc.shape[0]
        me = lax.axis_index('ei') * eo_size + lax.axis_index('eo')
        wg, wu, wd = w_gate[0], w_up[0], w_down[0]
        x = lax.all_gather(tok_loc, GROUP, axis=0, tiled=True)
        ids = lax.all_gather(idx_loc, GROUP, axis=0, tiled=True)
        gates = lax.all_gather(gate_loc, GROUP, axis=0, tiled=True)
        dy = lax.all_gather(dy_loc, GROUP, axis=0, tiled=True)
        hit = ids == me
        mask = jnp.any(hit, axis=1)[:, None]
        gate = jnp.sum(jnp.where(hit, gates, 0.0), axis=1)[:, None]
        a = dot(x, wg, ((1,), (0,)))
        b = dot(x, wu, ((1,), (0,)))
        s = jax.nn.sigmoid(a)
        h = jnp.where(mask, a * s * b, 0.0).astype(bf16)
        o = dot(h, wd, ((1,), (0,))).astype(bf16)
        y = lax.psum_scatter(gate * o.astype(f32), GROUP, scatter_dimension=0, tiled=True).astype(bf16)
        dyf = dy.astype(f32)
        dgate = jnp.sum(dyf * o.astype(f32), axis=1).reshape(-1, tok_dev)
        dgate = lax.all_gather(dgate[None], GROUP, axis=0, tiled=True)[:, me]
        dgate = jnp.take_along_axis(dgate.T, idx_loc, axis=1)
        u = (gate * dyf).astype(bf16)
        q = dot(u, wd, ((1,), (1,)))
        du = jnp.where(mask, q * a * s, 0.0).astype(bf16)
        dg = jnp.where(mask, q * b * s * (1.0 + a * (1.0 - s)), 0.0).astype(bf16)
        dx = (dot(dg, wg, ((1,), (1,))) + dot(du, wu, ((1,), (1,)))).astype(bf16)
        dx = lax.psum_scatter(dx.astype(f32), GROUP, scatter_dimension=0, tiled=True).astype(bf16)
        dwg = dot(x, dg, ((0,), (0,))).astype(bf16)[None]
        dwu = dot(x, du, ((0,), (0,))).astype(bf16)[None]
        dwd = dot(h, u, ((0,), (0,))).astype(bf16)[None]
        return y, dx, dgate, dwg, dwu, dwd

    return jax.shard_map(device_step, mesh=mesh, in_specs=(tok_spec, tok_spec, tok_spec, exp_spec, exp_spec, exp_spec, tok_spec), out_specs=(tok_spec,) * 6, check_vma=False)
```

time: 2500 us -> 838 us (0.34)
  waiting for transfers between devices: 1700 us -> 258 us
  local copies, waits for them, and re-layouts: 319 us -> 111 us
  blocking collectives: 0 us -> 101 us
  other arithmetic: 78.3 us -> 3.22 us
  starting transfers between devices: 67.6 us -> 0.25 us
    all_to_all x8 -> x0, waiting for transfers between devices: 1700 us -> none  [the longest x4 870 us: exchange(): peer_grid = lax.all_to_all(peer_grid, 'eo', 1, 1, tiled=True)]
    reduce_scatter x0 -> x1, waiting for transfers between devices: none -> 174 us  [device_step(): lax.psum_scatter(dx.astype(f32), GROUP, scatter_dimension=0, tiled=True)]
    gather x8 -> x5, local copies, waits for them, and re-layouts: 155 us -> 13.1 us  [device_step(): dgate = jnp.take_along_axis(dgate.T, idx_loc, axis=1)]
    all_gather x0 -> x3, blocking collectives: none -> 101 us  [the longest x1 34 us: device_step(): ids = lax.all_gather(idx_loc, GROUP, axis=0, tiled=True)]
    all_to_all x4 -> x0, local copies, waits for them, and re-layouts: 84.1 us -> none  [exchange(): peer_grid = lax.all_to_all(peer_grid, 'eo', 1, 1, tiled=True)]
    all_gather x0 -> x2, waiting for transfers between devices: none -> 82 us  [the longest x1 55.3 us: device_step(): x = lax.all_gather(tok_loc, GROUP, axis=0, tiled=True)]
    all_to_all x8 -> x0, starting transfers between devices: 67.6 us -> none  [the longest x4 34.9 us: exchange(): peer_grid = lax.all_to_all(peer_grid, 'ei', 0, 0, tiled=True)]
    another operation x4 -> x1, local copies, waits for them, and re-layouts: 63.2 us -> 0.07 us  [device_step(): dgate = lax.all_gather(dgate[None], GROUP, axis=0, tiled=True)[:, me]]
  transfers between devices with their start and end apart: 8 -> 4, of which waited for: 8 -> 3; matrix products, arithmetic and copies ran while one was open for 19% -> 30% of each run, Pallas kernels for 0% -> 0%
where the time goes in v1:
time: 838 us; the launch traced here: 831 us
  matrix products  344 us (41%)
  waiting for transfers between devices  258 us (31%)
  local copies, waits for them, and re-layouts  111 us (13%)
  blocking collectives  101 us (12%)
  between operations  14.3 us (2%)
    dot_general x9, matrix products, dot(): return lax.dot_general(x, y, (dims, ((), ())), preferred_element_type=f32)  344 us
    reduce_scatter x1, waiting for transfers between devices, device_step(): lax.psum_scatter(dx.astype(f32), GROUP, scatter_dimension=0, tiled=True)  174 us
    unnamed x16, local copies, waits for them, and re-layouts  65.1 us
    all_gather x1, waiting for transfers between devices, device_step(): x = lax.all_gather(tok_loc, GROUP, axis=0, tiled=True)  55.3 us
    all_gather x1, blocking collectives, device_step(): ids = lax.all_gather(idx_loc, GROUP, axis=0, tiled=True)  34 us
    all_gather x1, blocking collectives, device_step(): gates = lax.all_gather(gate_loc, GROUP, axis=0, tiled=True)  33.4 us
    all_gather x1, blocking collectives, device_step(): dgate = lax.all_gather(dgate[None], GROUP, axis=0, tiled=True)[:, me]  33.2 us
    all_gather x1, local copies, waits for them, and re-layouts, device_step(): dy = lax.all_gather(dy_loc, GROUP, axis=0, tiled=True)  32.9 us
  transfers between devices with their start and end apart: 4, of which 3 were waited for; matrix products, arithmetic and copies ran while one was open for 30% of the time, Pallas kernels for 0%

profile of v1, /device:TPU:97, one launch (start us, length us, event | category | flops | bytes accessed | tf_op | source)
XLA Modules:
  0.0 831.1 jit_solution(2092741697989234003)
XLA Ops:
  8.0 0.7 all-gather.5.cloned.1.call-update
  8.9 33.4 %all-gather.1 = f32[32,192,8]{1,2,0:T(8,128)S(1)} all-gather(f32[1,192,8]{1,2,0:T(8,128)} %bitcast.54), channel_id=1, replica_groups=mesh['dp'=1,'ei'=4,'eo'=8] {'ei','eo'}, dimensions={0}, use_global_device_ids=true | all-gather | bytes 202752 | tf_op jit(solution)/shard_map/all_gather | solution.py:24
  42.3 34.0 %all-gather = s32[32,192,8]{1,2,0:T(8,128)S(1)} all-gather(s32[1,192,8]{1,2,0:T(8,128)} %bitcast.53), channel_id=1, replica_groups=mesh['dp'=1,'ei'=4,'eo'=8] {'ei','eo'}, dimensions={0}, use_global_device_ids=true | all-gather | bytes 202752 | tf_op jit(solution)/shard_map/all_gather | solution.py:23
  76.7 26.7 %all-gather.7.cloned.1.call-done = bf16[6144,2048]{1,0:T(8,128)(2,1)} async-done(((bf16[192,2048]{1,0:T(8,128)(2,1)}), bf16[6144,2048]{1,0:T(8,128)(2,1)}) %all-gather.7.cloned.1.call-update) | async-done | bytes 25165840 | tf_op jit(solution)/shard_map/all_gather | solution.py:25
  103.4 32.9 %copy.37 = bf16[6144,2048]{0,1:T(8,128)(2,1)} copy(bf16[6144,2048]{1,0:T(8,128)(2,1)} %all-gather.7.cloned.1.call-done) | data formatting | bytes 50331648 | tf_op jit(solution)/shard_map/all_gather | solution.py:25
  136.3 55.3 %all-gather.5.cloned.1.call-done = bf16[6144,2048]{1,0:T(8,128)(2,1)} async-done(((bf16[192,2048]{1,0:T(8,128)(2,1)}), bf16[6144,2048]{1,0:T(8,128)(2,1)}) %all-gather.5.cloned.1.call-update) | async-done | bytes 25165840 | tf_op jit(solution)/shard_map/all_gather | solution.py:22
  191.5 33.1 %fusion.10 = f32[6144,1024]{1,0:T(8,128)} fusion(bf16[6144,2048]{1,0:T(8,128)(2,1)} %all-gather.5.cloned.1.call-done, bf16[1,2048,1024]{2,1,0:T(8,128)(2,1)} %param.11), kind=kOutput, calls=%fused_computation.18 | convolution fusion | flops 25769803776 | bytes 54525952 | tf_op jit(solution)/shard_map/dot_general | solution.py:16
  224.6 32.8 %fusion.14 = f32[6144,1024]{1,0:T(8,128)} fusion(bf16[6144,2048]{1,0:T(8,128)(2,1)S(1)} %copy-done.4, bf16[1,2048,1024]{2,1,0:T(8,128)(2,1)} %param.10), kind=kOutput, calls=%fused_computation.22 | convolution fusion | flops 25769803776 | bytes 54525952 | tf_op jit(solution)/shard_map/dot_general | solution.py:16
  257.4 49.7 %select_convert_fusion = (bf16[6144,1024]{1,0:T(8,128)(2,1)}, bf16[6144,1024]{1,0:T(8,128)(2,1)}, bf16[6144,1024]{1,0:T(8,128)(2,1)}) fusion(f32[6144,1024]{1,0:T(8,128)} %fusion.14, pred[6144]{0:T(1024)(128)(4,1)S(1)} %reshape.41, f32[6144,1024]{1,0:T(8,128)} %fusion.10, bf16[1,1024,2048]{2,1,0:T(8,128)(2,1)} %param.12, bf16[6144,2048]{0,1:T(8,128)(2,1)} %copy.37, ...), kind=kOutput, calls=%fused_computation.7 | convolution fusion | flops 25927090176 | bytes 117471232 | tf_op jit(solution)/shard_map/dot_general | solution.py:16
  307.1 40.7 %fusion.1 = (f32[6144]{0:T(1024)}, f32[6144,2048]{0,1:T(8,128)}) fusion(bf16[6144,2048]{0,1:T(8,128)(2,1)} %copy.37, f32[6144]{0:T(1024)S(1)} %reshape.44, bf16[6144,1024]{1,0:T(8,128)(2,1)} %get-tuple-element.34, bf16[1,1024,2048]{2,1,0:T(8,128)(2,1)} %param.12), kind=kOutput, calls=%fused_computation.5 | convolution fusion | flops 25845295104 | bytes 92323840 | tf_op jit(solution)/shard_map/dot_general | solution.py:16
  347.8 48.9 %copy.43 = f32[6144,2048]{1,0:T(8,128)} copy(f32[6144,2048]{0,1:T(8,128)} %get-tuple-element.36) | data formatting | bytes 100663296
  396.8 34.9 %fusion.12 = f32[6144,2048]{1,0:T(8,128)} fusion(bf16[6144,1024]{1,0:T(8,128)(2,1)} %get-tuple-element.33, bf16[1,2048,1024]{2,1,0:T(8,128)(2,1)} %param.10), kind=kOutput, calls=%fused_computation.20 | convolution fusion | flops 25769803776 | bytes 67108864 | tf_op jit(solution)/shard_map/dot_general | solution.py:16
  431.7 49.8 %fusion.2 = f32[6144,2048]{1,0:T(8,128)} fusion(f32[6144,2048]{1,0:T(8,128)} %fusion.12, bf16[6144,1024]{1,0:T(8,128)(2,1)} %get-tuple-element.32, bf16[1,2048,1024]{2,1,0:T(8,128)(2,1)} %param.11), kind=kOutput, calls=%fused_computation.12 | convolution fusion | flops 25807552512 | bytes 117440512 | tf_op jit(solution)/shard_map/dot_general | solution.py:16
  482.4 34.4 %convert_bitcast_fusion.2 = bf16[1,2048,1024]{1,2,0:T(8,128)(2,1)} fusion(bf16[6144,1024]{1,0:T(8,128)(2,1)} %get-tuple-element.33, bf16[6144,2048]{1,0:T(8,128)(2,1)} %all-gather.5.cloned.1.call-done), kind=kOutput, calls=%fused_computation.26 | convolution fusion | flops 25771900928 | bytes 41943040 | tf_op jit(solution)/shard_map/dot_general | solution.py:16
  516.7 6.4 copy.41
  523.1 34.2 %convert_bitcast_fusion.1 = bf16[1,2048,1024]{1,2,0:T(8,128)(2,1)} fusion(bf16[6144,1024]{1,0:T(8,128)(2,1)} %get-tuple-element.32, bf16[6144,2048]{1,0:T(8,128)(2,1)} %all-gather.5.cloned.1.call-done), kind=kOutput, calls=%fused_computation.25 | convolution fusion | flops 25771900928 | bytes 41943040 | tf_op jit(solution)/shard_map/dot_general | solution.py:16
  557.3 6.4 copy.42
  563.8 33.2 %all_gather.19 = f32[32,32,192]{2,1,0:T(8,128)S(1)} all-gather(f32[1,32,192]{2,1,0:T(8,128)S(1)} %broadcast_in_dim_reshape.3), channel_id=1, replica_groups=mesh['dp'=1,'ei'=4,'eo'=8] {'ei','eo'}, dimensions={0}, use_global_device_ids=true | all-gather | bytes 811008 | tf_op jit(solution)/shard_map/all_gather | solution.py:37
  597.1 12.7 %gather_fusion = f32[1536]{0:T(1024)S(1)} fusion(f32[192,32]{0,1:T(8,128)S(1)} %bitcast.52, s32[1536]{0:T(1024)S(1)} %reshape.24), kind=kCustom, calls=%fused_computation | custom fusion | bytes 24576 | tf_op jit(solution)/shard_map/jit(take_along_axis)/gather | solution.py:38
  610.6 34.3 %convert_bitcast_fusion = bf16[1,1024,2048]{2,1,0:T(8,128)(2,1)} fusion(bf16[6144,1024]{1,0:T(8,128)(2,1)} %get-tuple-element.34, bf16[6144,2048]{0,1:T(8,128)(2,1)} %copy.37, f32[6144]{0:T(1024)S(1)} %copy-done.2), kind=kOutput, calls=%fused_computation.24 | convolution fusion | flops 25809649664 | bytes 41967616 | tf_op jit(solution)/shard_map/dot_general | solution.py:16
  644.9 1.6 copy.44
  646.5 1.2 copy.40
  647.7 174.1 %reduce-scatter.5.cloned.1.call-done = f32[192,2048]{1,0:T(8,128)} async-done(((f32[6144,2048]{1,0:T(8,128)}), f32[192,2048]{1,0:T(8,128)}) %reduce-scatter.5.cloned.1.call-update) | async-done | bytes 1572880 | tf_op jit(solution)/shard_map/reduce_scatter | solution.py:44
  821.8 2.4 convert_element_type.59
  (31 shorter events, 3.2 us)
Async XLA Ops:
  7.2 96.2 %all-gather.7.cloned.1.call-start = ((), (), s32[]{:S(2)}) async-start(), calls=%async_computation.3 | async-start | bytes 25952256 | tf_op jit(solution)/shard_map/all_gather | solution.py:25
  8.0 183.6 %all-gather.5.cloned.1.call-start = ((), (), s32[]{:S(2)}) async-start(), calls=%async_computation.2 | async-start | bytes 25952256 | tf_op jit(solution)/shard_map/all_gather | solution.py:22
  8.8 636.1 %reduce-scatter.7.cloned.1.call-start = ((), (), s32[]{:S(2)}) async-start(), calls=%async_computation.5 | async-start | bytes 51904512
  76.5 230.6 %copy-start.1 = (f32[6144]{0:T(1024)}, f32[6144]{0:T(1024)S(1)}, u32[]{:S(2)}) copy-start(f32[6144]{0:T(1024)S(1)} %reshape.44) | copy-start | bytes 73732
  191.5 33.1 %copy-start.4 = (bf16[6144,2048]{1,0:T(8,128)(2,1)S(1)}, bf16[6144,2048]{1,0:T(8,128)(2,1)}, u32[]{:S(2)}) copy-start(bf16[6144,2048]{1,0:T(8,128)(2,1)} %all-gather.5.cloned.1.call-done) | copy-start | bytes 75497472
  396.7 425.1 %reduce-scatter.5.cloned.1.call-start = ((), (), s32[]{:S(2)}) async-start(), calls=%async_computation.4 | async-start | bytes 51904512 | tf_op jit(solution)/shard_map/reduce_scatter | solution.py:44
  481.4 0.7 copy-start
  523.1 40.5 %copy-start.3 = (f32[6144]{0:T(1024)S(1)}, f32[6144]{0:T(1024)}, u32[]{:S(2)}) copy-start(f32[6144]{0:T(1024)} %get-tuple-element.35) | copy-start | bytes 73732
  597.0 13.5 %copy-start.2 = (f32[6144]{0:T(1024)S(1)}, f32[6144]{0:T(1024)}, u32[]{:S(2)}) copy-start(f32[6144]{0:T(1024)} %copy-done.1) | copy-start | bytes 73732
Sparse Core Ops, SparseCore 0:
  10.1 93.2 all-gather.6
  105.5 86.0 all-gather.4
  396.8 211.9 reduce-scatter.6
  612.5 209.2 reduce-scatter.4

commit v2 on v1

v2 whole, which is shorter than its diff:
```python
import functools
import jax
import jax.numpy as jnp
from jax import lax
from jax.experimental import pallas as pl
from jax.experimental.pallas import tpu as pltpu
from jax.sharding import PartitionSpec as P

LANES, SUBLANES = 128, 8
MESH = pl.DeviceIdType.MESH
RING = 4
BACK = RING - 1
KK = (0, 1)
HOPS = ((0, 1), (0, -1), (1, 1), (1, -1))
NEIGHBOURS = ((1, 0), (BACK, 0), (0, 1), (0, BACK))
ANY = pl.BlockSpec(memory_space=pl.ANY)
f32, bf16 = jnp.float32, jnp.bfloat16
VMEM_LIMIT = 62 * 1024 * 1024


class Place:
    def __init__(self, tok_dev, half):
        self.dp, self.y, eo = lax.axis_index('dp'), lax.axis_index('ei'), lax.axis_index('eo')
        self.x, self.c = eo // 2, eo % 2
        self.tok_dev, self.half = tok_dev, half

    def chip(self, r1, r2, c=None):
        c = self.c if c is None else c
        dx, dy = (1 - c) * r1 + c * r2, (1 - c) * r2 + c * r1
        return (self.y + dy) % RING, (self.x + dx) % RING

    def device(self, r1, r2):
        y, x = self.chip(r1, r2)
        return (self.dp, y, 2 * x + self.c)

    def partner(self):
        return (self.dp, self.y, 2 * self.x + 1 - self.c)

    def rows(self, r1, r2, kk, c=None):
        c = self.c if c is None else c
        y, x = self.chip(r1, r2, c)
        return pl.ds(pl.multiple_of(((y * RING + x) * 2 + (c + kk) % 2) * self.tok_dev, self.tok_dev), self.tok_dev)

    def cols(self, mine=True):
        return pl.ds(pl.multiple_of((self.c if mine else 1 - self.c) * self.half, self.half), self.half)

    def greet(self):
        barrier = pltpu.get_barrier_semaphore()
        peers = [self.partner()] + [self.device(*r) for r in NEIGHBOURS]
        for peer in peers:
            pl.semaphore_signal(barrier, inc=1, device_id=peer, device_id_type=MESH)
        pl.semaphore_wait(barrier, len(peers))


def hops(r):
    return min(r, RING - r)


def ag_order():
    chips = sorted(((r1, r2) for r1 in range(RING) for r2 in range(RING)), key=lambda r: (hops(r[0]) + hops(r[1]), r[1]))[1:]
    near = len(NEIGHBOURS)
    return [(*r, kk) for kk in KK for r in chips[:near]] + [(*r, kk) for r in chips[near:] for kk in KK]


class Gather:
    N_SEMS = 5

    def __init__(self, place, loc, out, send, recv, d2d_send, d2d_recv, misc):
        self.p, self.loc, self.out = place, loc, out
        self.send, self.recv, self.d2d_send, self.d2d_recv, self.misc = send, recv, d2d_send, d2d_recv, misc

    @staticmethod
    def scratch():
        s = pltpu.SemaphoreType.DMA
        return [s((2, 2, RING, RING, 2)), s((RING, RING, 2)), s((RING, RING, 2)), s((RING, RING, 2)), s((3,))]

    def piece(self, r1, r2, kk):
        return self.out.at[self.p.rows(r1, r2, kk), self.p.cols()]

    def hop(self, axis, step, r1, r2, kk, src=None):
        to = (step % RING, 0) if axis == 0 else (0, step % RING)
        t1, t2 = (r1 - to[0]) % RING, (r2 - to[1]) % RING
        dst = self.piece(r1, r2, kk)
        return pltpu.make_async_remote_copy(
            src_ref=dst if src is None else src, dst_ref=dst, send_sem=self.send.at[axis, (1 - step) // 2, r1, r2, kk],
            recv_sem=self.recv.at[t1, t2, kk], device_id=self.p.device(*to), device_id_type=MESH)

    def arrived(self, r1, r2, kk):
        ref = self.piece(r1, r2, kk)
        pltpu.make_async_copy(ref, ref, self.recv.at[r1, r2, kk]).wait()

    def d2d(self, r1, r2, kk):
        ref = self.piece(r1, r2, kk)
        return pltpu.make_async_remote_copy(src_ref=ref, dst_ref=ref, send_sem=self.d2d_send.at[r1, r2, kk],
                                            recv_sem=self.d2d_recv.at[r1, r2, kk], device_id=self.p.partner(), device_id_type=MESH)

    def own(self):
        p = self.p
        rows = p.rows(0, 0, 0)
        local = pltpu.make_async_copy(self.loc, self.out.at[rows], self.misc.at[0])
        swap = pltpu.make_async_remote_copy(src_ref=self.loc, dst_ref=self.out.at[rows], send_sem=self.misc.at[1],
                                            recv_sem=self.misc.at[2], device_id=p.partner(), device_id_type=MESH)
        return local, swap

    def begin(self):
        local, swap = self.own()
        swap.start()
        src = self.loc.at[:, self.p.cols()]
        for axis, step in HOPS:
            self.hop(axis, step, 0, 0, 0, src).start()
        local.start()

    def begin_partner(self):
        ref = self.out.at[self.p.rows(0, 0, 1)]
        pltpu.make_async_copy(ref, ref, self.misc.at[2]).wait()
        for axis, step in HOPS:
            self.hop(axis, step, 0, 0, 1).start()

    def sends_of(self, r1, r2, kk):
        if r1 == r2 == 0:
            return HOPS
        onward = [h for h, r, k in zip(HOPS[::2] + HOPS[1::2], (r1, r2) * 2, (0, 0, 1, 1)) if (r, k) == (BACK if k == 0 else 1, kk)]
        if r2 == 0:
            return [h for h in onward if h[0] == 0] + list(HOPS[2:])
        return [h for h in onward if h[0] == 1]

    def relay(self, r1, r2, kk):
        self.arrived(r1, r2, kk)
        for axis, step in self.sends_of(r1, r2, kk):
            self.hop(axis, step, r1, r2, kk).start()
        self.d2d(r1, r2, kk).start()

    def finish(self):
        local, swap = self.own()
        local.wait()
        swap.wait_send()
        src = self.loc.at[:, self.p.cols()]
        for kk in KK:
            for axis, step in self.sends_of(0, 0, kk):
                self.hop(axis, step, 0, 0, kk, src if kk == 0 else None).wait_send()
        for r1, r2, kk in ag_order():
            for axis, step in self.sends_of(r1, r2, kk):
                self.hop(axis, step, r1, r2, kk).wait_send()
            self.d2d(r1, r2, kk).wait_send()
            ref = self.out.at[self.p.rows(r1, r2, kk, 1 - self.p.c), self.p.cols(False)]
            pltpu.make_async_copy(ref, ref, self.d2d_recv.at[r1, r2, kk]).wait()


def ag_kernel(loc, table, out, table_out, *sems):
    gs = [Gather(Place(r.shape[0], r.shape[1] // 2), r, o, *sems[k * Gather.N_SEMS:(k + 1) * Gather.N_SEMS])
          for k, (r, o) in enumerate(((table, table_out), (loc, out)))]
    gs[0].p.greet()
    for g in gs:
        g.begin()
    for g in gs:
        g.begin_partner()
    for piece in ag_order():
        for g in gs:
            g.relay(*piece)
    for g in gs:
        g.finish()


def all_gather_rows(loc, table, group, cid):
    return pl.pallas_call(
        ag_kernel, out_shape=[jax.ShapeDtypeStruct((group * r.shape[0], r.shape[1]), r.dtype) for r in (loc, table)],
        in_specs=[ANY] * 2, out_specs=[ANY] * 2, scratch_shapes=Gather.scratch() * 2,
        compiler_params=pltpu.CompilerParams(collective_id=cid, has_side_effects=True), name='gather_rows')(loc, table)


LEGS = {'far': lambda d: (2, d, 0), 'near': lambda d: (1 + 2 * d, 1 - d, 2 - d), 'pass': lambda d: (1 + 2 * d, d, 1 + d)}


def rs_group(kind, r=None):
    ops = []
    arrived = lambda q, kk: [(q, d, 1 + kk) for d in KK]
    for d in KK:
        if kind == 'final':
            ops.append(dict(chip=(0, 0), kk=d, recvs=arrived(0, d) + arrived(RING, d), axis=None))
            continue
        off, kk, slot = LEGS[kind](d)
        q = RING if r is None else r
        recvs = [(q, d, 0)] if kind == 'pass' else []
        if r is None:
            ops.append(dict(chip=(off, 0), kk=kk, recvs=arrived(off, kk) + recvs, axis=0, step=1 - 2 * d, dst=(q, d, slot)))
        else:
            ops.append(dict(chip=(r, off), kk=kk, recvs=recvs, axis=1, step=1 - 2 * d, dst=(q, d, slot)))
    return ops


def rs_groups():
    order = [('far', 2), ('near', 2), ('far', 1), ('pass', 2), ('near', 1), ('far', BACK), ('pass', 1), ('near', BACK), ('far', 0), ('pass', BACK),
             ('far',), ('near', 0), ('pass', 0), ('near',), ('pass',), ('final',)]
    return [rs_group(*k) for k in order]


SLOTS = 8


class Scatter:
    def __init__(self, place, own, po, rbuf, out, gates, scratch):
        self.p, self.own, self.po, self.rbuf, self.out, self.gates = place, own, po, rbuf, out, gates
        (self.slots, self.in_o, self.in_p, self.in_r, self.fin, self.send, self.recv, self.d2d_send, self.d2d_recv, self.load,
         self.fin_sem) = scratch
        self.groups = rs_groups()
        self.n = 0
        for grp in self.groups:
            for op in grp:
                if op['axis'] is not None:
                    op['n'] = self.n
                    self.n += 1
        self.by_n = {op['n']: op for grp in self.groups for op in grp if op['axis'] is not None}

    @staticmethod
    def scratch(tok, half):
        s = pltpu.SemaphoreType.DMA
        return [pltpu.VMEM((SLOTS, tok, half), f32), pltpu.VMEM((2, tok, half), bf16), pltpu.VMEM((2, tok, half), bf16),
                pltpu.VMEM((2, 4, tok, half), f32), pltpu.VMEM((2, tok, half), bf16),
                s((30,)), s((RING + 1, 2, 3)), s((RING, RING, 2)), s((RING, RING, 2)), s((2, 6)), s((3,))]

    @staticmethod
    def hbm(tok, half, group):
        return [jax.ShapeDtypeStruct((group * tok, half), bf16), jax.ShapeDtypeStruct((RING + 1, 2, 3, tok, half), f32)]

    def swap(self, op):
        k = (*op['chip'], op['kk'])
        rows = self.p.rows(*k, 1 - self.p.c)
        return pltpu.make_async_remote_copy(
            src_ref=self.own.at[rows, self.p.cols(False)], dst_ref=self.po.at[rows], send_sem=self.d2d_send.at[k],
            recv_sem=self.d2d_recv.at[k], device_id=self.p.partner(), device_id_type=MESH)

    def begin(self):
        for grp in self.groups:
            for op in grp:
                self.swap(op).start()

    def loads(self, j, op):
        rows = self.p.rows(*op['chip'], op['kk'])
        out = [pltpu.make_async_copy(self.own.at[rows, self.p.cols()], self.in_o.at[j], self.load.at[j, 0]),
               pltpu.make_async_copy(self.po.at[rows], self.in_p.at[j], self.load.at[j, 1])]
        for i, r in enumerate(op['recvs']):
            out.append(pltpu.make_async_copy(self.rbuf.at[r], self.in_r.at[j, i], self.load.at[j, 2 + i]))
        return out

    def prep(self, g):
        for j, op in enumerate(self.groups[g]):
            k = (*op['chip'], op['kk'])
            rows = self.p.rows(*k)
            pltpu.make_async_copy(self.po.at[rows], self.po.at[rows], self.d2d_recv.at[k]).wait()
            for r in op['recvs']:
                pltpu.make_async_copy(self.rbuf.at[r], self.rbuf.at[r], self.recv.at[r]).wait()
            for copy in self.loads(j, op):
                copy.start()

    def sender(self, op):
        to = (op['step'] % RING, 0) if op['axis'] == 0 else (0, op['step'] % RING)
        return pltpu.make_async_remote_copy(
            src_ref=self.slots.at[op['n'] % SLOTS], dst_ref=self.rbuf.at[op['dst']], send_sem=self.send.at[op['n']],
            recv_sem=self.recv.at[op['dst']], device_id=self.p.device(*to), device_id_type=MESH)

    def fire(self, g):
        tok = self.p.tok_dev
        step = 32
        for j, op in enumerate(self.groups[g]):
            for copy in self.loads(j, op):
                copy.wait()
            sent = op['axis'] is not None
            if sent and op['n'] >= SLOTS:
                self.sender(self.by_n[op['n'] - SLOTS]).wait_send()
            y, x = self.p.chip(*op['chip'])
            row0 = ((y * RING + x) * 2 + (self.p.c + op['kk']) % 2) * tok

            def body(i, _):
                rows = pl.ds(pl.multiple_of(i * step, step), step)
                v = self.in_o[j, rows].astype(f32)
                w = self.in_p[j, rows].astype(f32)
                if self.gates is not None:
                    at = pl.ds(pl.multiple_of(row0 + i * step, step), step)
                    v = v * self.gates[at, 0:1]
                    w = w * self.gates[at, 2:3]
                v = v + w
                for r in range(len(op['recvs'])):
                    v = v + self.in_r[j, r, rows]
                if sent:
                    self.slots[op['n'] % SLOTS, rows] = v
                else:
                    self.fin[j, rows] = v.astype(bf16)
                return 0
            lax.fori_loop(0, tok // step, body, 0)
            if sent:
                self.sender(op).start()

    def result(self):
        dst = self.out.at[:, self.p.cols()]
        local = pltpu.make_async_copy(self.fin.at[0], dst, self.fin_sem.at[0])
        swap = pltpu.make_async_remote_copy(src_ref=self.fin.at[1], dst_ref=dst, send_sem=self.fin_sem.at[1], recv_sem=self.fin_sem.at[2],
                                            device_id=self.p.partner(), device_id_type=MESH)
        return local, swap

    def finish(self):
        local, swap = self.result()
        local.start()
        swap.start()
        for n in range(max(0, self.n - SLOTS), self.n):
            self.sender(self.by_n[n]).wait_send()
        for grp in self.groups:
            for op in grp:
                self.swap(op).wait_send()
        local.wait()
        swap.wait_send()
        ref = self.out.at[:, self.p.cols(False)]
        pltpu.make_async_copy(ref, ref, self.fin_sem.at[2]).wait()

    def before(self, step, at):
        @pl.when(step == 0)
        def _():
            self.p.greet()
            self.begin()
            self.prep(0)
            self.fire(0)
        for g in range(1, len(self.groups)):
            pl.when(step == at[g])(functools.partial(self.prep, g))

    def after(self, step, at):
        for g in range(1, len(self.groups)):
            pl.when(step == at[g])(functools.partial(self.fire, g))
        pl.when(step == at[-1])(self.finish)


def mm(x, y, cx, cy):
    return lax.dot_general(x, y, (((cx,), (cy,)), ((), ())), preferred_element_type=f32)


def forward_kernel(at, x, gm, wg, wu, wd, dy_loc, a_out, b_out, h_out, o_out, dy_out, *sems):
    i = pl.program_id(0)
    place = Place(dy_loc.shape[0], dy_loc.shape[1] // 2)
    g = Gather(place, dy_loc, dy_out, *sems)

    @pl.when(i == 0)
    def _():
        place.greet()
        g.begin()
        g.begin_partner()
    pieces = ag_order()
    for s in sorted(set(at)):
        @pl.when(i == s)
        def _():
            for piece, t in zip(pieces, at):
                if t == s:
                    g.relay(*piece)
    mask = gm[:, 1:2] > 0.0
    ff = wg.shape[1]
    n = ff // 2
    for k in range(2):
        cs = slice(k * n, (k + 1) * n)
        a = mm(x[...], wg[:, cs], 1, 0)
        b = mm(x[...], wu[:, cs], 1, 0)
        a_out[:, cs] = a
        b_out[:, cs] = b
        h_out[:, cs] = jnp.where(mask, a * jax.nn.sigmoid(a) * b, 0.0).astype(bf16)
    o_out[...] = mm(h_out[...], wd[...], 1, 0).astype(bf16)

    @pl.when(i == pl.num_programs(0) - 1)
    def _():
        g.finish()


FWD_LAST, BWD_LAST, WTS_LAST = 19, 21, 15


def schedule(steps, last):
    n = len(rs_groups())
    return [0] + [g * last // (n - 3) for g in range(n - 2)] + [steps - 1]


def rows_spec(tile, width):
    return pl.BlockSpec((tile, width), lambda i: (i, 0))


def whole_spec(shape):
    return pl.BlockSpec(shape, lambda i: (0,) * len(shape), pipeline_mode=pl.Buffered(1))


def params(cid):
    return pltpu.CompilerParams(collective_id=cid, has_side_effects=True, vmem_limit_bytes=VMEM_LIMIT, dimension_semantics=('arbitrary',))


def forward(x, gm, wg, wu, wd, dy_loc, cid, tile=256):
    n_tok, d = x.shape
    ff = wg.shape[1]
    steps = n_tok // tile
    at = [1 + k * FWD_LAST // len(ag_order()) for k in range(len(ag_order()))]
    S = jax.ShapeDtypeStruct
    return pl.pallas_call(
        functools.partial(forward_kernel, at), grid=(steps,),
        out_shape=[S((n_tok, ff), f32), S((n_tok, ff), f32), S((n_tok, ff), bf16), S((n_tok, d), bf16), S((n_tok, d), bf16)],
        in_specs=[rows_spec(tile, d), rows_spec(tile, gm.shape[1]), whole_spec(wg.shape), whole_spec(wu.shape), whole_spec(wd.shape), ANY],
        out_specs=[rows_spec(tile, ff), rows_spec(tile, ff), rows_spec(tile, ff), rows_spec(tile, d), ANY],
        scratch_shapes=Gather.scratch(), compiler_params=params(cid), name='forward')(x, gm, wg, wu, wd, dy_loc)


def backward_kernel(at, dy, gm, a, b, o, wg, wu, wd, gates, o_any, dg_out, du_out, u_out, dx_out, dgate_out, y_out, po, rbuf, *scratch):
    i = pl.program_id(0)
    tok, half = y_out.shape[0], y_out.shape[1] // 2
    rs = Scatter(Place(tok, half), o_any, po, rbuf, y_out, gates, scratch)
    rs.before(i, at)
    mask = gm[:, 1:2] > 0.0
    dyf = dy[...].astype(f32)
    u_out[...] = (gm[:, 0:1] * dyf).astype(bf16)
    dgate_out[...] = jnp.sum(dyf * o[...].astype(f32), axis=1, keepdims=True)
    n = wg.shape[1] // 2
    for k in range(2):
        cs = slice(k * n, (k + 1) * n)
        q = mm(u_out[...], wd[cs, :], 1, 1)
        av, bv = a[:, cs], b[:, cs]
        s = jax.nn.sigmoid(av)
        qs = q * s
        du_out[:, cs] = jnp.where(mask, q * av * s, 0.0).astype(bf16)
        dg_out[:, cs] = jnp.where(mask, q * bv * s * (1.0 + av * (1.0 - s)), 0.0).astype(bf16)
    dx_out[...] = (mm(dg_out[...], wg[...], 1, 1) + mm(du_out[...], wu[...], 1, 1)).astype(bf16)
    rs.after(i, at)


def backward(dy, gm, a, b, o, wg, wu, wd, tok, cid, tile=256):
    n_tok, d = dy.shape
    ff = wg.shape[1]
    steps = n_tok // tile
    at = schedule(steps, BWD_LAST)
    S = jax.ShapeDtypeStruct
    hbm = Scatter.hbm(tok, d // 2, n_tok // tok)
    out = pl.pallas_call(
        functools.partial(backward_kernel, at), grid=(steps,),
        out_shape=[S((n_tok, ff), bf16), S((n_tok, ff), bf16), S((n_tok, d), bf16), S((n_tok, d), bf16), S((n_tok, 1), f32), S((tok, d), bf16)] + hbm,
        in_specs=[rows_spec(tile, d), rows_spec(tile, gm.shape[1]), rows_spec(tile, ff), rows_spec(tile, ff), rows_spec(tile, d),
                  whole_spec(wg.shape), whole_spec(wu.shape), whole_spec(wd.shape), whole_spec(gm.shape), ANY],
        out_specs=[rows_spec(tile, ff), rows_spec(tile, ff), rows_spec(tile, d), rows_spec(tile, d), rows_spec(tile, 1), ANY, ANY, ANY],
        scratch_shapes=Scatter.scratch(tok, d // 2), compiler_params=params(cid), name='backward')(dy, gm, a, b, o, wg, wu, wd, gm, o)
    return out[:6]


def weights_kernel(at, n_k, x, dg, du, h, u, dx_any, dgate, dwg, dwu, dwd, dxs_out, dgate_out, po, rbuf, acc, stage, out_sem, *scratch):
    i = pl.program_id(0)
    tok, half = dxs_out.shape[0], dxs_out.shape[1] // 2
    rs = Scatter(Place(tok, half), dx_any, po, rbuf, dxs_out, None, scratch[Gather.N_SEMS:])
    rs.before(i, at)
    small = Gather(Place(dgate.shape[0], dgate.shape[1] // 2), dgate, dgate_out, *scratch[:Gather.N_SEMS])
    pieces = ag_order()
    far = [hops(r1) + hops(r2) for r1, r2, _ in pieces]
    pl.when(i == 0)(small.begin)
    pl.when(i == 1)(small.begin_partner)
    for k in sorted(set(far)):
        @pl.when(i == (3 * n_k - 2) * k // max(far))
        def _():
            for piece, n in zip(pieces, far):
                if n == k:
                    small.relay(*piece)
    pl.when(i == 3 * n_k - 1)(small.finish)
    ff = dg.shape[1]
    m = 256

    def flush(w, dst):
        return pltpu.make_async_copy(stage, dst, out_sem)

    def flush_d(k):
        return pltpu.make_async_copy(stage.at[pl.ds(k * ff, ff)], dwd.at[:, pl.ds(k * ff, ff)], out_sem)

    kc = i % n_k

    @pl.when(kc == 0)
    def _():
        def zero(r, _):
            acc[pl.ds(pl.multiple_of(r * 64, 64), 64)] = jnp.zeros((64, acc.shape[1]), f32)
            return 0
        lax.fori_loop(0, acc.shape[0] // 64, zero, 0)

    def add(left, right, row0=0, cols=None):
        def tile(r, _):
            lc = pl.ds(pl.multiple_of(r * m, m), m)
            rows = pl.ds(pl.multiple_of(row0 + r * m, m), m)
            acc[rows] += mm(left[:, lc], right[...] if cols is None else right[:, cols], 0, 0)
            return 0
        lax.fori_loop(0, left.shape[1] // m, tile, 0)

    pl.when(i < n_k)(lambda: add(x, dg))
    pl.when((i >= n_k) & (i < 2 * n_k))(lambda: add(x, du))

    @pl.when(i >= 2 * n_k)
    def _():
        for k in range(2):
            add(h, u, k * ff, slice(k * ff, (k + 1) * ff))

    @pl.when(i == 2 * n_k - 1)
    def _():
        flush(0, dwg).wait()

    @pl.when(i == 3 * n_k - 1)
    def _():
        flush(1, dwu).wait()

    @pl.when(kc == n_k - 1)
    def _():
        def conv(r, _):
            rows = pl.ds(pl.multiple_of(r * 64, 64), 64)
            stage[rows] = acc[rows].astype(bf16)
            return 0
        lax.fori_loop(0, acc.shape[0] // 64, conv, 0)

    pl.when(i == n_k - 1)(lambda: flush(0, dwg).start())
    pl.when(i == 2 * n_k - 1)(lambda: flush(1, dwu).start())

    @pl.when(i == 3 * n_k - 1)
    def _():
        flush_d(0).start()
        flush_d(1).start()
    rs.after(i, at)

    @pl.when(i == 3 * n_k - 1)
    def _():
        flush_d(0).wait()
        flush_d(1).wait()


def weights(x, dg, du, h, u, dx, dgate, tok, cid, tile=1024):
    n_tok, d = x.shape
    ff = dg.shape[1]
    n_k = n_tok // tile
    steps = 3 * n_k
    last = n_k - 1
    at = schedule(steps, WTS_LAST)
    S = jax.ShapeDtypeStruct
    hbm = Scatter.hbm(tok, d // 2, n_tok // tok)
    spec = lambda width, index: pl.BlockSpec((tile, width), lambda i: (index(i), 0))
    out = pl.pallas_call(
        functools.partial(weights_kernel, at, n_k), grid=(steps,),
        out_shape=[S((d, ff), bf16), S((d, ff), bf16), S((ff, d), bf16), S((tok, d), bf16), S((n_tok // tok * dgate.shape[0], dgate.shape[1]), f32)] + hbm,
        in_specs=[spec(d, lambda i: jnp.where(i < n_k, i, jnp.minimum(i - n_k, last))), spec(ff, lambda i: jnp.minimum(i, last)),
                  spec(ff, lambda i: jnp.clip(i - n_k, 0, last)), spec(ff, lambda i: jnp.maximum(i - 2 * n_k, 0)),
                  spec(d, lambda i: jnp.maximum(i - 2 * n_k, 0)), ANY, ANY],
        out_specs=[ANY] * 7,
        scratch_shapes=[pltpu.VMEM((d, ff), f32), pltpu.VMEM((d, ff), bf16), pltpu.SemaphoreType.DMA] + Gather.scratch() + Scatter.scratch(tok, d // 2),
        compiler_params=params(cid), name='weights')(x, dg, du, h, u, dx, dgate)
    return out[:5]


def solution(mesh):
    eo_size = mesh.shape['eo']
    group = mesh.shape['ei'] * eo_size
    tok_spec = P(('dp', 'ei', 'eo'))
    exp_spec = P(('ei', 'eo'))

    def device_step(tok_loc, idx_loc, gate_loc, w_gate, w_up, w_down, dy_loc):
        tok_dev, top_k = idx_loc.shape
        me = lax.axis_index('ei') * eo_size + lax.axis_index('eo')
        mate = me + 1 - 2 * (me % 2)
        wg, wu, wd = w_gate[0], w_up[0], w_down[0]
        n_val, wide = tok_dev * top_k, 2 * LANES
        table = jnp.concatenate([idx_loc.astype(f32).reshape(-1), gate_loc.reshape(-1)])
        n_row = -(-table.shape[0] // (wide * SUBLANES)) * SUBLANES
        table = jnp.pad(table, (0, n_row * wide - table.shape[0])).reshape(n_row, wide)
        x, table = all_gather_rows(tok_loc, table, group, 0)
        table = table.reshape(group, -1)
        ids, gates = table[:, :n_val].reshape(-1, top_k), table[:, n_val:2 * n_val].reshape(-1, top_k)

        def column(e):
            hit = ids == e.astype(f32)
            return jnp.sum(jnp.where(hit, gates, 0.0), axis=1), jnp.any(hit, axis=1).astype(f32)
        gm = jnp.stack(column(me) + column(mate), axis=1)
        a, b, h, o, dy = forward(x, gm, wg, wu, wd, dy_loc, 1)
        dg, du, u, dx, dgate, y = backward(dy, gm, a, b, o, wg, wu, wd, tok_dev, 2)
        dgate = dgate.reshape(-1, wide)
        dwg, dwu, dwd, dxs, dgate = weights(x, dg, du, h, u, dx, dgate, tok_dev, 3)
        dgate = lax.dynamic_index_in_dim(dgate.reshape(group, group, tok_dev), me, 1, keepdims=False)
        expert = jnp.arange(group, dtype=jnp.int32)[:, None, None]
        dgate = jnp.sum(jnp.where(idx_loc[None] == expert, dgate[:, :, None], 0.0), axis=0)
        return y, dxs, dgate, dwg[None], dwu[None], dwd[None]

    return jax.shard_map(device_step, mesh=mesh, in_specs=(tok_spec, tok_spec, tok_spec, exp_spec, exp_spec, exp_spec, tok_spec), out_specs=(tok_spec,) * 6, check_vma=False)
```

time: 838 us -> 545 us (0.65)
  Pallas kernels: 0 us -> 508 us
  matrix products: 344 us -> 0 us
  waiting for transfers between devices: 258 us -> 0 us
  blocking collectives: 101 us -> 0 us
  local copies, waits for them, and re-layouts: 111 us -> 26.4 us
  between operations: 14.3 us -> 0.85 us
    pallas_call x0 -> x4, Pallas kernels: none -> 508 us  [the longest x1 158 us: weights(): pl.pallas_call(functools.partial(weights_kernel, at, n_k), grid=(steps,),...]
    dot_general x9 -> x0, matrix products: 344 us -> none  [dot(): return lax.dot_general(x, y, (dims, ((), ())), preferred_element_type=f32)]
    reduce_scatter x1 -> x0, waiting for transfers between devices: 174 us -> none  [device_step(): lax.psum_scatter(dx.astype(f32), GROUP, scatter_dimension=0, tiled=True)]
    all_gather x3 -> x0, blocking collectives: 101 us -> none  [the longest x1 34 us: device_step(): ids = lax.all_gather(idx_loc, GROUP, axis=0, tiled=True)]
    all_gather x2 -> x0, waiting for transfers between devices: 82 us -> none  [the longest x1 55.3 us: device_step(): x = lax.all_gather(tok_loc, GROUP, axis=0, tiled=True)]
    unnamed x16 -> x19, local copies, waits for them, and re-layouts: 65.1 us -> 14.3 us
    all_gather x1 -> x0, local copies, waits for them, and re-layouts: 32.9 us -> none  [device_step(): dy = lax.all_gather(dy_loc, GROUP, axis=0, tiled=True)]
    gather x5 -> x0, local copies, waits for them, and re-layouts: 13.1 us -> none  [device_step(): dgate = jnp.take_along_axis(dgate.T, idx_loc, axis=1)]
  transfers between devices with their start and end apart: 4 -> 0, of which waited for: 3 -> 0; matrix products, arithmetic and copies ran while one was open for 30% -> 0% of each run, Pallas kernels for 0% -> 0%
where the time goes in v2:
time: 545 us
  Pallas kernels  508 us (93%)
  local copies, waits for them, and re-layouts  26.4 us (5%)
  other arithmetic  9.16 us (2%)
    pallas_call x1, Pallas kernels, weights(): pl.pallas_call(functools.partial(weights_kernel, at, n_k), grid=(steps,),...  158 us
    pallas_call x1, Pallas kernels, backward(): pl.pallas_call(functools.partial(backward_kernel, at), grid=(steps,), out...  152 us
    pallas_call x1, Pallas kernels, forward(): pl.pallas_call(functools.partial(forward_kernel, at), grid=(steps,), out_...  116 us
    pallas_call x1, Pallas kernels, all_gather_rows(): pl.pallas_call(ag_kernel, out_shape=[jax.ShapeDtypeStruct((group * r.shap...  81.8 us
    unnamed x19, local copies, waits for them, and re-layouts  14.3 us

profile of v2, /device:TPU:97, one launch (start us, length us, event | category | flops | bytes accessed | tf_op | source)
XLA Modules:
  0.0 544.7 jit_solution(8040116415422757367)
XLA Ops:
  0.6 0.7 convert_element_type.37
  1.6 0.8 copy.28
  3.1 81.8 %gather_rows.1 = (bf16[6144,2048]{1,0:T(8,128)(2,1)}, f32[512,256]{1,0:T(8,128)}) custom-call(bf16[192,2048]{1,0:T(8,128)(2,1)} %loc.1, f32[16,256]{1,0:T(8,128)} %reshape.61.table), custom_call_target="tpu_custom_call" | custom-call | tf_op jit(solution)/shard_map/gather_rows/pallas_call | solution.py:165
  84.9 1.1 reshape.62
  86.1 1.9 eq.35
  88.0 0.9 reduce_or.18
  89.0 1.9 eq.38
  90.9 0.9 reduce_or.19
  91.8 1.7 reshape.63
  93.5 3.1 select_reduce_fusion.1
  96.7 2.4 copy.29.gm.gates
  99.1 115.6 %forward.1 = (f32[6144,1024]{1,0:T(8,128)}, f32[6144,1024]{1,0:T(8,128)}, bf16[6144,1024]{1,0:T(8,128)(2,1)}, bf16[6144,2048]{1,0:T(8,128)(2,1)}, bf16[6144,2048]{1,0:T(8,128)(2,1)}) custom-call(bf16[6144,2048]{1,0:T(8,128)(2,1)} %get-tuple-element.24.x, f32[6144,4]{1,0:T(8,128)} %copy.29.gm.gates, bf16[2048,1024]{1,0:T(8,128)(2,1)} %bitcast.13, ...), custom_call_target="tpu_custom_call" | custom-call | tf_op jit(solution)/shard_map/forward/pallas_call | solution.py:394
  214.7 152.4 %backward.1 = (bf16[6144,1024]{1,0:T(8,128)(2,1)}, bf16[6144,1024]{1,0:T(8,128)(2,1)}, bf16[6144,2048]{1,0:T(8,128)(2,1)}, bf16[6144,2048]{1,0:T(8,128)(2,1)}, f...) custom-call(bf16[6144,2048]{1,0:T(8,128)(2,1)} %get-tuple-element.26, ...), custom_call_target="tpu_custom_call" | custom-call | tf_op jit(solution)/shard_map/backward/pallas_call | solution.py:431
  367.1 2.8 reduce
  369.8 0.6 reshape.64.dgate
  370.5 158.5 %weights.1 = (bf16[2048,1024]{1,0:T(8,128)(2,1)}, bf16[2048,1024]{1,0:T(8,128)(2,1)}, bf16[1024,2048]{1,0:T(8,128)(2,1)}, bf16[192,2048]{1,0:T(8,128)(2,1)}, f32...) custom-call(bf16[6144,2048]{1,0:T(8,128)(2,1)} %get-tuple-element.24.x, ...), custom_call_target="tpu_custom_call" | custom-call | tf_op jit(solution)/shard_map/weights/pallas_call | solution.py:533
  529.0 1.5 reshape.65
  530.5 0.6 select_reduce_fusion.2
  531.2 0.9 copy.40
  532.1 2.1 copy.41
  534.1 4.8 copy.42
  539.0 2.1 copy.43
  541.1 1.6 copy-done.2
  542.7 2.0 copy.44
  (23 shorter events, 1.2 us)
Async XLA Ops:
  88.0 3.7 copy-start
  90.9 0.9 copy-start.1
  370.5 160.1 %copy-start.5 = (s32[192,8]{0,1:T(8,128)S(1)}, s32[192,8]{0,1:T(8,128)}, u32[]{:S(2)}) copy-start(s32[192,8]{0,1:T(8,128)} %param.8) | copy-start | bytes 18436
  370.5 160.7 %copy-start.4 = (bf16[192,2048]{1,0:T(8,128)(2,1)S(1)}, bf16[192,2048]{1,0:T(8,128)(2,1)}, u32[]{:S(2)}) copy-start(bf16[192,2048]{1,0:T(8,128)(2,1)} %get-tuple-element.52) | copy-start | bytes 2359300
  534.1 4.8 copy-start.3
  539.0 3.7 copy-start.2
